TPU v7x, 32 devices: a whole 2x2x4 slice. The times are simulated.
32 devices in a mesh: row: 2 (over y), theta: 4 (over x, core), gz: 4 (over z).
Axes of the slice: x: 2, y: 2, z: 4, core: 2. Of those that a mesh axis runs over, the one named last changes fastest.
Arguments:
- state_start: float32 [6, 8, 128, 1024], P(None, 'row', 'gz', 'theta'), may hold values from -1.2 to 1.2
- state_section: float32 [6, 8, 128, 1024], P(None, 'row', 'gz', 'theta'), may hold values from -1.5 to 4, as said below
- phase: int32 [8, 128, 1024], P('row', 'gz', 'theta'), may hold values 0 or 1
- cutoff: int32 [4], replicated, may hold values from 1 to 63
Outputs:
- state_next: float32 [6, 8, 128, 1024], P(None, 'row', 'gz', 'theta')
Inputs may be any that keep to these rules, and one draw needn't show every extreme that they name: `state_section`: channel 0 (density) lies in 0.5 to 2.0, channels 1 to 3 (momenta) in -1.5 to 1.5, channel 4 (total energy) in 2.5 to 4.0, channel 5 (jet mass density) in 0 to 1.0.
All inputs are finite; a program needn't handle non-finite values. No bound on the sum of `phase` on one device may be relied on, other than what follows from the above.
Results may differ from a plain program's by a relative error of at most 0.0003.
Values sent between devices are 32-bit elements; how exact they have to be, the bound alone decides.
A program may use at most 64 MiB of HBM per device.

v0:
```python
import math
import jax
import jax.numpy as jnp
from jax import lax
from jax.sharding import PartitionSpec as P

NT = 1024
KMODES = 64
split_speed = 10.0
time_step = 0.05
weno_epsilon = 1e-06
liquid_ratio = 4.4
gas_ratio = 1.4
liquid_stiffness = 0.6


def passed_along(value, axis, steps):
    count = lax.axis_size(axis)
    pairs = [(source, (source + steps) % count) for source in range(count)]
    return lax.ppermute(value, axis, pairs)


def with_halo(cells, sides, width):
    for axis, dim in sides:
        count = lax.axis_size(axis)
        head = lax.slice_in_dim(cells, 0, width, axis=dim)
        tail = lax.slice_in_dim(cells, cells.shape[dim] - width, cells.shape[dim], axis=dim)
        cells = jnp.concatenate(
            [
                lax.ppermute(tail, axis, [(i, (i + 1) % count) for i in range(count)]),
                cells,
                lax.ppermute(head, axis, [((i + 1) % count, i) for i in range(count)]),
            ],
            axis=dim,
        )
    return cells


def pressure_of(state, phase):
    density = state[0]
    kinetic = 0.5 * (state[1] * state[1] + state[2] * state[2] + state[3] * state[3]) / density
    liquid = phase == 1
    heat_ratio = jnp.where(liquid, liquid_ratio, gas_ratio)
    stiffness = jnp.where(liquid, liquid_stiffness, 0.0)
    return (heat_ratio - 1.0) * (state[4] - kinetic) - heat_ratio * stiffness


def weno_face(far_left, near_left, centre, near_right, far_right):
    smooth_left = (
        13.0 / 12.0 * (far_left - 2.0 * near_left + centre) ** 2
        + 0.25 * (far_left - 4.0 * near_left + 3.0 * centre) ** 2
    )
    smooth_mid = (
        13.0 / 12.0 * (near_left - 2.0 * centre + near_right) ** 2
        + 0.25 * (near_left - near_right) ** 2
    )
    smooth_right = (
        13.0 / 12.0 * (centre - 2.0 * near_right + far_right) ** 2
        + 0.25 * (3.0 * centre - 4.0 * near_right + far_right) ** 2
    )
    weight_left = 0.1 / (weno_epsilon + smooth_left) ** 2
    weight_mid = 0.6 / (weno_epsilon + smooth_mid) ** 2
    weight_right = 0.3 / (weno_epsilon + smooth_right) ** 2
    weight_sum = weight_left + weight_mid + weight_right
    value_left = (2.0 * far_left - 7.0 * near_left + 11.0 * centre) / 6.0
    value_mid = (-near_left + 5.0 * centre + 2.0 * near_right) / 6.0
    value_right = (2.0 * centre + 5.0 * near_right - far_right) / 6.0
    return (
        weight_left * value_left + weight_mid * value_mid + weight_right * value_right
    ) / weight_sum


def face_fluxes(padded_line, array_axis, component):
    density = padded_line[0]
    velocity = padded_line[component] / density
    pressure_field = padded_line[6]
    conserved = padded_line[:6]
    flux_rows = [conserved[channel] * velocity for channel in range(6)]
    flux_rows[component] = flux_rows[component] + pressure_field
    flux_rows[4] = flux_rows[4] + pressure_field * velocity
    physical = jnp.stack(flux_rows)
    upward = 0.5 * (physical + split_speed * conserved)
    downward = 0.5 * (physical - split_speed * conserved)
    face_count = padded_line.shape[array_axis] - 5

    def shifted(values, offset):
        return lax.slice_in_dim(values, offset, offset + face_count, axis=array_axis)

    upwind_part = weno_face(
        shifted(upward, 0),
        shifted(upward, 1),
        shifted(upward, 2),
        shifted(upward, 3),
        shifted(upward, 4),
    )
    downwind_part = weno_face(
        shifted(downward, 5),
        shifted(downward, 4),
        shifted(downward, 3),
        shifted(downward, 2),
        shifted(downward, 1),
    )
    return upwind_part + downwind_part


def tendency(centre_cells, radial_line, axial_line, azimuth_line, cycle_start):
    cycle_count = centre_cells.shape[1]
    radial_flux = face_fluxes(radial_line, 1, 1)
    axial_flux = face_fluxes(axial_line, 2, 3)
    azimuth_flux = face_fluxes(azimuth_line, 3, 2)
    cycle_index = (cycle_start + lax.iota(jnp.int32, cycle_count + 1)).astype(centre_cells.dtype)
    face_radius = cycle_index[None, :, None, None]
    cell_radius = face_radius[:, :-1] + 0.5
    weighted = face_radius * radial_flux
    div_radial = (weighted[:, 1:] - weighted[:, :-1]) / cell_radius
    div_axial = axial_flux[:, :, 1:] - axial_flux[:, :, :-1]
    angle_step = 2.0 * math.pi / NT
    div_azimuth = (azimuth_flux[..., 1:] - azimuth_flux[..., :-1]) / (cell_radius * angle_step)
    density = centre_cells[0]
    swirl_speed = centre_cells[2] / density
    radius = cell_radius[0]
    source_radial = (centre_cells[2] * swirl_speed + centre_cells[6]) / radius
    source_swirl = -centre_cells[1] * swirl_speed / radius
    zero_field = jnp.zeros_like(density)
    source = jnp.stack(
        [zero_field, source_radial, source_swirl, zero_field, zero_field, zero_field]
    )
    return source - div_radial - div_axial - div_azimuth


def across_axis(partner):
    sign_flip = jnp.array([1.0, -1.0, -1.0, 1.0, 1.0, 1.0, 1.0], partner.dtype)[:, None, None, None]
    return partner[:, ::-1] * sign_flip


def build_table(positions, mode_count, length):
    orders = lax.iota(jnp.int32, mode_count)
    phases = positions[:, None] * orders[None, :] % length
    angles = phases.astype(jnp.float32) * (2.0 * math.pi / length)
    return jnp.concatenate([jnp.cos(angles), jnp.sin(angles)], 1)


def cycle_weights(cutoff, mode_count, length):
    orders = lax.iota(jnp.int32, mode_count)
    mode_scale = jnp.where(orders == 0, 1.0 / length, 2.0 / length)
    kept_modes = orders[None, :] <= cutoff[:, None]
    weight_half = jnp.where(kept_modes, mode_scale[None, :], 0.0)
    return jnp.concatenate([weight_half, weight_half], 1)


def apply_filter(cycle_block, weights, theta_id):
    local_theta = cycle_block.shape[3]
    positions = theta_id * local_theta + lax.iota(jnp.int32, local_theta)
    fourier_table = build_table(positions, KMODES, NT)
    coefficients = jnp.einsum(
        "vizt,tk->vizk", cycle_block, fourier_table, precision=lax.Precision.HIGHEST
    )
    coefficients = lax.psum(coefficients, "theta")
    coefficients = coefficients * weights[None, :, None, :]
    return jnp.einsum("vizk,tk->vizt", coefficients, fourier_table, precision=lax.Precision.HIGHEST)


def shards(state_start, state_section, phase, cutoff):
    row_count = lax.axis_size("row")
    row_id = lax.axis_index("row")
    theta_count = lax.axis_size("theta")
    theta_id = lax.axis_index("theta")
    cycle_count = state_section.shape[1]
    filtered_count = cutoff.shape[0]
    pressure_field = pressure_of(state_section, phase)
    fields = jnp.concatenate([state_section, pressure_field[None]], 0)
    partner = passed_along(fields[:, 0:3], "theta", theta_count // 2)
    mirror = across_axis(partner)
    outer_rim = jnp.repeat(fields[:, -1:], 3, axis=1)
    padded = with_halo(fields, (("row", 1), ("theta", 3), ("gz", 2)), 3)
    radial_line = padded[:, :, 3:-3, 3:-3]
    axial_line = padded[:, 3:-3, :, 3:-3]
    azimuth_line = padded[:, 3:-3, 3:-3, :]
    lower_rim = jnp.where(row_id == 0, mirror, radial_line[:, :3])
    upper_rim = jnp.where(row_id == row_count - 1, outer_rim, radial_line[:, -3:])
    radial_line = jnp.concatenate([lower_rim, fields, upper_rim], 1)
    tendencies = tendency(fields, radial_line, axial_line, azimuth_line, row_id * cycle_count)
    advanced = 0.75 * state_start + 0.25 * (state_section + time_step * tendencies)
    weights = cycle_weights(cutoff, KMODES, NT)
    filtered = apply_filter(advanced, weights, theta_id)
    inner_next = jnp.where(row_id == 0, filtered, advanced)
    return jnp.concatenate([inner_next, advanced[:, filtered_count:]], 1)


def solution(mesh):
    in_specs = (
        P(None, "row", "gz", "theta"),
        P(None, "row", "gz", "theta"),
        P("row", "gz", "theta"),
        P(),
    )
    out_specs = P(None, "row", "gz", "theta")
    return jax.shard_map(shards, mesh=mesh, in_specs=in_specs, out_specs=out_specs, check_vma=False)
```

profile of v0, /device:TPU:0, one launch (start us, length us, event | category | flops | bytes accessed | tf_op | source)
XLA Modules:
  0.0 148.2 jit_solution(16903499594754744437)
XLA Ops:
  6.6 1.4 bitcast_dynamic-update-slice_fusion
  8.0 1.2 fusion.11
  9.2 3.0 %collective-permute-start.2 = (f32[7,3,32,256]{3,2,1,0:T(8,128)}, f32[7,3,32,256]{3,2,1,0:T(8,128)S(1)}, u32[]{:S(2)}, u32[]{:S(2)}) collective-permute-start(f32[7,3,32,256]{3,2,1,0:T(8,128)} %get-tuple-element.24), channel_id=1, source_target_pairs={{16,0},{0,16},{17,1},{1,17},{18,2},{2,18},{19,3},{3,19},{20,4},{4,... | collective-permute-start | bytes 2064392 | tf_op jit(solution)/shard_map/ppermute | solution.py:32
  12.2 1.5 %collective-permute-start = (f32[7,3,32,256]{3,2,1,0:T(8,128)}, f32[7,3,32,256]{3,2,1,0:T(8,128)}, u32[]{:S(2)}, u32[]{:S(2)}) collective-permute-start(f32[7,3,32,256]{3,2,1,0:T(8,128)} %get-tuple-element.24), channel_id=1, source_target_pairs={{0,8},{4,12},{8,0},{12,4},{1,9},{5,13},{9,1},{13,5},{2,10},{6,14},... | collective-permute-start | bytes 2064392 | tf_op jit(solution)/shard_map/ppermute | solution.py:20
  13.7 0.5 collective-permute-start.1
  14.2 0.1 divide_dynamic-update-slice_fusion
  14.5 0.6 fusion.47
  15.1 13.7 %collective-permute-done.2 = f32[7,3,32,256]{3,2,1,0:T(8,128)S(1)} collective-permute-done((f32[7,3,32,256]{3,2,1,0:T(8,128)}, f32[7,3,32,256]{3,2,1,0:T(8,128)S(1)}, u32[]{:S(2)}, u32[]{:S(2)}) %collective-permute-start.2) | collective-permute-done | bytes 688160 | tf_op jit(solution)/shard_map/ppermute | solution.py:32
  28.8 13.8 %collective-permute-done.1 = f32[7,3,32,256]{3,2,1,0:T(8,128)S(1)} collective-permute-done((f32[7,3,32,256]{3,2,1,0:T(8,128)}, f32[7,3,32,256]{3,2,1,0:T(8,128)S(1)}, u32[]{:S(2)}, u32[]{:S(2)}) %collective-permute-start.1) | collective-permute-done | bytes 688160 | tf_op jit(solution)/shard_map/ppermute | solution.py:30
  42.6 1.5 %multiply_select_fusion = f32[7,3,32,256]{3,2,1,0:T(8,128)S(1)} fusion(f32[7,3,32,256]{3,2,1,0:T(8,128)S(1)} %collective-permute-done.1, f32[7,3,32,256]{3,2,1,0:T(8,128)} %collective-permute-done, f32[7]{0:T(128)S(1)} %copy-done.10, pred[]{:T(512)S(6)} %eq.25), kind=kLoop, calls=%fused_computation.37 | loop fusion | flops 344064 | bytes 2064413 | tf_op jit(solution)/shard_map/jit(_where)/select_n | solution.py:179
  44.2 1.9 %pad_maximum_fusion.2 = (f32[7,10,32,256]{3,2,1,0:T(8,128)}, f32[7,10,32,256]{3,2,1,0:T(8,128)S(1)}) fusion(f32[7,3,32,256]{3,2,1,0:T(8,128)S(1)} %broadcast_select_fusion, f32[1,4,32,256]{3,2,1,0:T(8,128)S(1)} %bitcast.49, f32[6,4,32,256]{3,2,1,0:T(8,128)S(1)} %copy-done, f32[7,3,32,256]{3,2,1,0:T(8,128)S(1)} %multiply_select_fusion, ...), kind=kLoop, calls=%fused_computation.2 | loop fusion | flops 2867200 | bytes 8257536 | tf_op jit(solution)/shard_map/concatenate | solution.py:181
  46.1 1.8 %fusion.56 = (f32[7,10,32,3]{3,2,1,0:T(8,128)}, f32[7,10,32,3]{3,2,1,0:T(8,128)}) fusion(f32[7,10,32,256]{3,2,1,0:T(8,128)S(1)} %get-tuple-element.22), kind=kLoop, calls=%fused_computation.127 | loop fusion | bytes 107520 | tf_op jit(solution)/shard_map/slice | solution.py:27
  47.9 2.6 %copy.7 = f32[7,10,32,3]{2,0,3,1:T(8,128)} copy(f32[7,10,32,3]{3,2,1,0:T(8,128)} %get-tuple-element.20) | data formatting | bytes 53760 | tf_op jit(solution)/shard_map/slice | solution.py:26
  50.5 0.3 collective-permute-start.4
  50.8 2.4 %copy.6 = f32[7,10,32,3]{2,0,3,1:T(8,128)} copy(f32[7,10,32,3]{3,2,1,0:T(8,128)} %get-tuple-element.19) | data formatting | bytes 53760 | tf_op jit(solution)/shard_map/slice | solution.py:27
  53.2 0.2 collective-permute-start.3
  53.8 0.7 add_multiply_fusion
  54.5 5.2 %add_multiply_fusion.3 = f32[6,5,32,256]{3,2,1,0:T(8,128)} fusion(f32[6,10,32,256]{3,2,1,0:T(8,128)S(1)} %get-tuple-element.16, f32[6,10,32,256]{3,2,1,0:T(8,128)S(1)} %get-tuple-element.15, f32[5]{0:T(128)S(1)} %add_convert_fusion), kind=kLoop, calls=%fused_computation.20 | loop fusion | flops 31948800 | bytes 10813460 | tf_op jit(solution)/shard_map/mul | solution.py:114
  59.7 1.4 copy.9
  61.1 1.4 copy.8
  62.5 2.6 %pad_maximum_fusion.1 = f32[7,10,32,262]{3,2,1,0:T(8,128)S(1)} fusion(f32[7,10,32,3]{3,2,1,0:T(8,128)S(1)} %copy.9, f32[7,3,32,256]{3,2,1,0:T(8,128)} %copy-done.3, f32[1,4,32,256]{3,2,1,0:T(8,128)S(1)} %bitcast.50, f32[6,4,32,256]{3,2,1,0:T(8,128)S(1)} %copy-done, f32[7,3,32,256]{3,2,1,0:T(8,128)} %copy-done.1, f32[7,10,32,3]{3,2,1,0:T(8,128)S(1)} %copy.8), kind=kLoop, calls=%fused_computation.1 | loop fusion | flops 2934400 | bytes 4695040 | tf_op jit(solution)/shard_map/concatenate | solution.py:28
  65.1 0.2 fusion.55
  65.2 0.9 copy-done.2
  66.1 0.2 copy-done.4
  66.4 0.2 multiply_dynamic-update-slice_fusion.1
  66.6 0.3 fusion.26
  66.8 0.3 fusion.25
  67.1 0.3 fusion.23
  67.4 0.3 fusion.22
  67.7 0.3 fusion.20
  68.0 0.3 add_multiply_fusion.1
  68.3 3.9 %collective-permute-start.6 = (f32[7,10,3,262]{3,2,1,0:T(4,128)S(1)}, f32[7,10,3,262]{3,2,1,0:T(4,128)S(1)}, u32[]{:S(2)}, u32[]{:S(2)}) collective-permute-start(f32[7,10,3,262]{3,2,1,0:T(4,128)S(1)} %get-tuple-element.18), channel_id=1, source_target_pairs={{1,0},{2,1},{3,2},{0,3},{5,4},{6,5},{7,6},{4,7},{9,8},{10,9},{11,1... | collective-permute-start | bytes 660248 | tf_op jit(solution)/shard_map/ppermute | solution.py:32
  72.2 5.9 %divide_add_fusion = f32[6,4,32,257]{3,2,1,0:T(8,128)S(1)} fusion(f32[6,4,32,262]{3,2,1,0:T(8,128)S(1)} %get-tuple-element.14, f32[6,4,32,262]{3,2,1,0:T(8,128)S(1)} %get-tuple-element.13), kind=kLoop, calls=%fused_computation.13 | loop fusion | flops 25461504 | bytes 8684544 | tf_op jit(solution)/shard_map/add | solution.py:103
  78.1 4.3 %collective-permute-done.6 = f32[7,10,3,262]{3,2,1,0:T(4,128)S(1)} collective-permute-done((f32[7,10,3,262]{3,2,1,0:T(4,128)S(1)}, f32[7,10,3,262]{3,2,1,0:T(4,128)S(1)}, u32[]{:S(2)}, u32[]{:S(2)}) %collective-permute-start.6) | collective-permute-done | bytes 220112 | tf_op jit(solution)/shard_map/ppermute | solution.py:32
  82.4 10.1 %collective-permute-done.5 = f32[7,10,3,262]{3,2,1,0:T(4,128)S(1)} collective-permute-done((f32[7,10,3,262]{3,2,1,0:T(4,128)S(1)}, f32[7,10,3,262]{3,2,1,0:T(4,128)S(1)}, u32[]{:S(2)}, u32[]{:S(2)}) %collective-permute-start.5) | collective-permute-done | bytes 220112 | tf_op jit(solution)/shard_map/ppermute | solution.py:30
  92.5 5.7 %pad_maximum_fusion = f32[7,10,38,262]{3,2,1,0:T(8,128)S(1)} fusion(f32[7,10,3,262]{3,2,1,0:T(4,128)S(1)} %collective-permute-done.6, f32[7,10,32,3]{3,2,1,0:T(8,128)S(1)} %copy.9, f32[7,3,32,256]{3,2,1,0:T(8,128)S(1)} %copy-done.4, f32[1,4,32,256]{3,2,1,0:T(8,128)S(1)} %bitcast.57, f32[6,4,32,256]{3,2,1,0:T(8,128)S(1)} %copy-done, ...), kind=kLoop, calls=%fused_computation | loop fusion | flops 4878440 | bytes 5575360 | tf_op jit(solution)/shard_map/concatenate | solution.py:28
  98.2 0.2 multiply_dynamic-update-slice_fusion.2
  98.4 0.1 fusion.32
  98.5 0.1 fusion.31
  98.6 0.2 add_dynamic-update-slice_fusion.1
  98.8 0.2 fusion.30
  98.9 0.1 fusion.28
  99.1 0.3 add_multiply_fusion.2
  99.4 5.0 %divide_add_fusion.1 = f32[6,4,33,256]{3,2,1,0:T(8,128)S(1)} fusion(f32[6,4,38,256]{3,2,1,0:T(8,128)S(1)} %get-tuple-element.12, f32[6,4,38,256]{3,2,1,0:T(8,128)S(1)} %get-tuple-element.11), kind=kLoop, calls=%fused_computation.17 | loop fusion | flops 26155008 | bytes 8921088 | tf_op jit(solution)/shard_map/add | solution.py:103
  104.5 0.7 fusion.7
  105.2 1.6 %fusion.48 = f32[6,4,32,128]{3,2,1,0:T(8,128)} fusion(f32[6,4,32,256]{3,2,1,0:T(8,128)S(1)} %fusion.7, f32[256,64]{1,0:T(8,128)S(1)} %get-tuple-element.26, f32[256,64]{1,0:T(8,128)S(1)} %get-tuple-element.25), kind=kOutput, calls=%fused_computation.112 | convolution fusion | flops 302022656 | bytes 1310720 | tf_op jit(solution)/shard_map/vizt,tk->vizk/dot_general | solution.py:155
  107.0 31.6 %all-reduce.2.cloned.1.call-done = f32[6,4,32,128]{3,2,1,0:T(8,128)} async-done(((f32[6,4,32,128]{3,2,1,0:T(8,128)}), f32[6,4,32,128]{3,2,1,0:T(8,128)}) %all-reduce.2.cloned.1.call-update) | async-done | bytes 393232 | tf_op jit(solution)/shard_map/psum | solution.py:158
  138.6 2.7 %convolution_select_fusion = f32[6,4,32,256]{3,2,1,0:T(8,128)} fusion(f32[6,4,32,256]{3,2,1,0:T(8,128)S(1)} %fusion.7, f32[6,4,32,128]{3,2,1,0:T(8,128)} %all-reduce.2.cloned.1.call-done, pred[]{:T(512)S(6)} %eq.25, f32[4,128]{1,0:T(4,128)S(1)} %pad_maximum_fusion.8, f32[256,64]{1,0:T(8,128)S(1)} %get-tuple-element.26, f32[256,64]{1,0:T(8,128)S(1)} %get-tuple-element.25), kind=kOutput, calls=%fused_computation.9 | convolution fusion | flops 302317568 | bytes 2099201 | tf_op jit(solution)/shard_map/vizk,tk->vizt/dot_general | solution.py:160
  (46 shorter events, 0.8 us)
Async XLA Ops:
  6.5 1.5 copy-start
  6.5 132.1 %all-reduce.2.cloned.1.call-start = ((), (), s32[]{:S(2)}) async-start(), calls=%async_computation | async-start | bytes 786432 | tf_op jit(solution)/shard_map/psum | solution.py:158
  9.2 19.5 %collective-permute-start.2 = (f32[7,3,32,256]{3,2,1,0:T(8,128)}, f32[7,3,32,256]{3,2,1,0:T(8,128)S(1)}, u32[]{:S(2)}, u32[]{:S(2)}) collective-permute-start(f32[7,3,32,256]{3,2,1,0:T(8,128)} %get-tuple-element.24), channel_id=1, source_target_pairs={{16,0},{0,16},{17,1},{1,17},{18,2},{2,18},{19,3},{3,19},{20,4},{4,... | collective-permute-start | bytes 2064392 | tf_op jit(solution)/shard_map/ppermute | solution.py:32
  12.2 30.4 %collective-permute-start = (f32[7,3,32,256]{3,2,1,0:T(8,128)}, f32[7,3,32,256]{3,2,1,0:T(8,128)}, u32[]{:S(2)}, u32[]{:S(2)}) collective-permute-start(f32[7,3,32,256]{3,2,1,0:T(8,128)} %get-tuple-element.24), channel_id=1, source_target_pairs={{0,8},{4,12},{8,0},{12,4},{1,9},{5,13},{9,1},{13,5},{2,10},{6,14},... | collective-permute-start | bytes 2064392 | tf_op jit(solution)/shard_map/ppermute | solution.py:20
  13.7 28.9 %collective-permute-start.1 = (f32[7,3,32,256]{3,2,1,0:T(8,128)}, f32[7,3,32,256]{3,2,1,0:T(8,128)S(1)}, u32[]{:S(2)}, u32[]{:S(2)}) collective-permute-start(f32[7,3,32,256]{3,2,1,0:T(8,128)} %get-tuple-element.23), channel_id=1, source_target_pairs={{0,16},{16,0},{1,17},{17,1},{2,18},{18,2},{3,19},{19,3},{4,20},{20... | collective-permute-start | bytes 2064392 | tf_op jit(solution)/shard_map/ppermute | solution.py:30
  14.4 28.2 %copy-start.10 = (f32[7]{0:T(128)S(1)}, f32[7]{0:T(128)}, u32[]{:S(2)}) copy-start(f32[7]{0:T(128)} %constant.69.clone) | copy-start | bytes 88
  14.4 29.7 %copy-start.7 = (f32[6,4,32,256]{3,2,1,0:T(8,128)}, f32[6,4,32,256]{3,2,1,0:T(8,128)S(1)}, u32[]{:S(2)}) copy-start(f32[6,4,32,256]{3,2,1,0:T(8,128)S(1)} %broadcast_dynamic-update-slice_fusion) | copy-start | bytes 2359300
  28.7 15.4 %copy-start.3 = (f32[7,3,32,256]{3,2,1,0:T(8,128)}, f32[7,3,32,256]{3,2,1,0:T(8,128)S(1)}, u32[]{:S(2)}) copy-start(f32[7,3,32,256]{3,2,1,0:T(8,128)S(1)} %collective-permute-done.2) | copy-start | bytes 2064388
  42.6 3.5 %copy-start.1 = (f32[7,3,32,256]{3,2,1,0:T(8,128)}, f32[7,3,32,256]{3,2,1,0:T(8,128)S(1)}, u32[]{:S(2)}) copy-start(f32[7,3,32,256]{3,2,1,0:T(8,128)S(1)} %collective-permute-done.1) | copy-start | bytes 2064388
  47.9 5.6 %copy-start.5 = (f32[7,10,32,256]{3,2,1,0:T(8,128)S(1)}, f32[7,10,32,256]{3,2,1,0:T(8,128)}, u32[]{:S(2)}) copy-start(f32[7,10,32,256]{3,2,1,0:T(8,128)} %get-tuple-element.21) | copy-start | bytes 6881284
  50.5 9.2 %collective-permute-start.4 = (f32[7,10,32,3]{2,0,3,1:T(8,128)}, f32[7,10,32,3]{2,0,3,1:T(8,128)}, u32[]{:S(2)}, u32[]{:S(2)}) collective-permute-start(f32[7,10,32,3]{2,0,3,1:T(8,128)} %copy.7), channel_id=1, source_target_pairs={{4,0},{8,4},{12,8},{0,12},{5,1},{9,5},{13,9},{1,13},{6,2},{10,6},{... | collective-permute-start | bytes 80648 | tf_op jit(solution)/shard_map/ppermute | solution.py:32
  53.2 7.9 %collective-permute-start.3 = (f32[7,10,32,3]{2,0,3,1:T(8,128)}, f32[7,10,32,3]{2,0,3,1:T(8,128)}, u32[]{:S(2)}, u32[]{:S(2)}) collective-permute-start(f32[7,10,32,3]{2,0,3,1:T(8,128)} %copy.6), channel_id=1, source_target_pairs={{0,4},{4,8},{8,12},{12,0},{1,5},{5,9},{9,13},{13,1},{2,6},{6,10},{... | collective-permute-start | bytes 80648 | tf_op jit(solution)/shard_map/ppermute | solution.py:30
  65.0 1.1 copy-start.2
  65.1 1.3 copy-start.4
  68.3 14.1 %collective-permute-start.6 = (f32[7,10,3,262]{3,2,1,0:T(4,128)S(1)}, f32[7,10,3,262]{3,2,1,0:T(4,128)S(1)}, u32[]{:S(2)}, u32[]{:S(2)}) collective-permute-start(f32[7,10,3,262]{3,2,1,0:T(4,128)S(1)} %get-tuple-element.18), channel_id=1, source_target_pairs={{1,0},{2,1},{3,2},{0,3},{5,4},{6,5},{7,6},{4,7},{9,8},{10,9},{11,1... | collective-permute-start | bytes 660248 | tf_op jit(solution)/shard_map/ppermute | solution.py:32
  72.2 20.3 %collective-permute-start.5 = (f32[7,10,3,262]{3,2,1,0:T(4,128)S(1)}, f32[7,10,3,262]{3,2,1,0:T(4,128)S(1)}, u32[]{:S(2)}, u32[]{:S(2)}) collective-permute-start(f32[7,10,3,262]{3,2,1,0:T(4,128)S(1)} %get-tuple-element.17), channel_id=1, source_target_pairs={{0,1},{1,2},{2,3},{3,0},{4,5},{5,6},{6,7},{7,4},{8,9},{9,10},{10,1... | collective-permute-start | bytes 660248 | tf_op jit(solution)/shard_map/ppermute | solution.py:30
  99.4 5.0 %copy-start.6 = (f32[6,5,32,256]{3,2,1,0:T(8,128)S(1)}, f32[6,5,32,256]{3,2,1,0:T(8,128)}, u32[]{:S(2)}) copy-start(f32[6,5,32,256]{3,2,1,0:T(8,128)} %add_multiply_fusion.3) | copy-start | bytes 2949124
  99.4 5.0 %copy-start.8 = (f32[6,4,32,256]{3,2,1,0:T(8,128)S(1)}, f32[6,4,32,256]{3,2,1,0:T(8,128)}, u32[]{:S(2)}) copy-start(f32[6,4,32,256]{3,2,1,0:T(8,128)} %copy-done.7) | copy-start | bytes 2359300
  99.4 5.0 %copy-start.9 = (f32[6,4,32,256]{3,2,1,0:T(8,128)S(1)}, f32[6,4,32,256]{3,2,1,0:T(8,128)}, u32[]{:S(2)}) copy-start(f32[6,4,32,256]{3,2,1,0:T(8,128)} %param.5) | copy-start | bytes 2359300
  105.2 1.6 %copy-start.11 = (s32[4]{0:T(128)S(1)}, s32[4]{0:T(128)}, u32[]{:S(2)}) copy-start(s32[4]{0:T(128)} %param.8) | copy-start | bytes 52
Sparse Core Ops, SparseCore 0:
  106.9 31.6 all-reduce.1
where the time goes:
time: 149 us; the launch traced here: 148 us
  waiting for transfers between devices  73.5 us (49%)
  other arithmetic  36.1 us (24%)
  between operations  13.8 us (9%)
  local copies, waits for them, and re-layouts  11 us (7%)
  starting transfers between devices  9.39 us (6%)
  matrix products  4.34 us (3%)
    psum x1, waiting for transfers between devices, apply_filter(): coefficients = lax.psum(coefficients, 'theta')  31.6 us
    ppermute x3, waiting for transfers between devices, with_halo(): lax.ppermute(tail, axis, [(i, (i + 1) % count) for i in range(count)])  23.9 us
    ppermute x3, waiting for transfers between devices, with_halo(): lax.ppermute(head, axis, [((i + 1) % count, i) for i in range(count)])  18 us
    add x2, other arithmetic, face_fluxes(): return upwind_part + downwind_part  10.9 us
    concatenate x2, other arithmetic, with_halo(): jnp.concatenate([lax.ppermute(tail, axis, [(i, (i + 1) % count) for i in...  8.27 us
    ppermute x3, starting transfers between devices, with_halo(): lax.ppermute(head, axis, [((i + 1) % count, i) for i in range(count)])  7.17 us
    mul x1, other arithmetic, tendency(): weighted = face_radius * radial_flux  5.18 us
    slice x3, local copies, waits for them, and re-layouts, with_halo(): lax.slice_in_dim(cells, cells.shape[dim] - width, cells.shape[dim], axis=...  4.38 us
  transfers between devices with their start and end apart: 8, of which 5 were waited for; matrix products, arithmetic and copies ran while one was open for 11% of the time, Pallas kernels for 0%

commit v1 on v0

--- a/solution.py
+++ b/solution.py
@@ -155,7 +155,11 @@
     coefficients = jnp.einsum(
         "vizt,tk->vizk", cycle_block, fourier_table, precision=lax.Precision.HIGHEST
     )
-    coefficients = lax.psum(coefficients, "theta")
+    coefficients = coefficients
+    for hop in (1, 2):
+        coefficients = coefficients + lax.ppermute(
+            coefficients, "theta", [(dev, dev ^ hop) for dev in range(4)]
+        )
     coefficients = coefficients * weights[None, :, None, :]
     return jnp.einsum("vizk,tk->vizt", coefficients, fourier_table, precision=lax.Precision.HIGHEST)
 

time: 149 us -> 115 us (0.77)
  waiting for transfers between devices: 73.5 us -> 53.6 us
  between operations: 13.8 us -> 0.39 us
  matrix products: 4.34 us -> 2.6 us
    psum x1 -> x0, waiting for transfers between devices: 31.6 us -> none  [apply_filter(): coefficients = lax.psum(coefficients, 'theta')]
    ppermute x0 -> x2, waiting for transfers between devices: none -> 11.7 us  [apply_filter(): lax.ppermute(coefficients, 'theta', [(dev, dev ^ hop) for dev in range(4)])]
  transfers between devices with their start and end apart: 8 -> 9, of which waited for: 5 -> 6; matrix products, arithmetic and copies ran while one was open for 11% -> 15% of each run, Pallas kernels for 0% -> 0%
where the time goes in v1:
time: 115 us; the launch traced here: 114 us
  waiting for transfers between devices  53.6 us (47%)
  other arithmetic  36.2 us (31%)
  local copies, waits for them, and re-layouts  11 us (10%)
  starting transfers between devices  10.5 us (9%)
  matrix products  2.6 us (2%)
    ppermute x3, waiting for transfers between devices, with_halo(): lax.ppermute(tail, axis, [(i, (i + 1) % count) for i in range(count)])  23.9 us
    ppermute x3, waiting for transfers between devices, with_halo(): lax.ppermute(head, axis, [((i + 1) % count, i) for i in range(count)])  18 us
    ppermute x2, waiting for transfers between devices, apply_filter(): lax.ppermute(coefficients, 'theta', [(dev, dev ^ hop) for dev in range(4)])  11.7 us
    add x2, other arithmetic, face_fluxes(): return upwind_part + downwind_part  10.9 us
    concatenate x2, other arithmetic, with_halo(): jnp.concatenate([lax.ppermute(tail, axis, [(i, (i + 1) % count) for i in...  8.27 us
    ppermute x3, starting transfers between devices, with_halo(): lax.ppermute(head, axis, [((i + 1) % count, i) for i in range(count)])  7.17 us
    mul x1, other arithmetic, tendency(): weighted = face_radius * radial_flux  5.2 us
    slice x3, local copies, waits for them, and re-layouts, with_halo(): lax.slice_in_dim(cells, cells.shape[dim] - width, cells.shape[dim], axis=...  4.38 us
  transfers between devices with their start and end apart: 9, of which 6 were waited for; matrix products, arithmetic and copies ran while one was open for 15% of the time, Pallas kernels for 0%

profile of v1, /device:TPU:0, one launch (start us, length us, event | category | flops | bytes accessed | tf_op | source)
XLA Modules:
  0.0 114.3 jit_solution(14251777406659594989)
XLA Ops:
  0.0 1.4 %bitcast_dynamic-update-slice_fusion = (f32[6,4,32,256]{3,2,1,0:T(8,128)S(1)}, f32[4,32,256]{2,1,0:T(8,128)S(1)}) fusion(f32[6,4,32,256]{3,2,1,0:T(8,128)S(1)} %broadcast_dynamic-update-slice_fusion.1, f32[6,4,32,256]{3,2,1,0:T(8,128)} %param.6, f32[4]{0:T(128)S(1)} %get-tuple-element.28, s32[4,32,256]{2,1,0:T(8,128)} %param.7), kind=kLoop, calls=%fused_computation.97 | loop fusion | flops 622592 | bytes 1049088
  1.5 1.2 %fusion.11 = (f32[7,3,32,256]{3,2,1,0:T(8,128)}, f32[7,3,32,256]{3,2,1,0:T(8,128)}) fusion(f32[6,4,32,256]{3,2,1,0:T(8,128)S(1)} %copy-done, f32[1,4,32,256]{3,2,1,0:T(8,128)S(1)} %bitcast.47), kind=kLoop, calls=%fused_computation.35 | loop fusion | flops 344064 | bytes 2293760 | tf_op jit(solution)/shard_map/concatenate | solution.py:175
  2.7 3.0 %collective-permute-start.2 = (f32[7,3,32,256]{3,2,1,0:T(8,128)}, f32[7,3,32,256]{3,2,1,0:T(8,128)S(1)}, u32[]{:S(2)}, u32[]{:S(2)}) collective-permute-start(f32[7,3,32,256]{3,2,1,0:T(8,128)} %get-tuple-element.24), channel_id=1, source_target_pairs={{16,0},{0,16},{17,1},{1,17},{18,2},{2,18},{19,3},{3,19},{20,4},{4,... | collective-permute-start | bytes 2064392 | tf_op jit(solution)/shard_map/ppermute | solution.py:32
  5.7 1.5 %collective-permute-start = (f32[7,3,32,256]{3,2,1,0:T(8,128)}, f32[7,3,32,256]{3,2,1,0:T(8,128)}, u32[]{:S(2)}, u32[]{:S(2)}) collective-permute-start(f32[7,3,32,256]{3,2,1,0:T(8,128)} %get-tuple-element.24), channel_id=1, source_target_pairs={{0,8},{4,12},{8,0},{12,4},{1,9},{5,13},{9,1},{13,5},{2,10},{6,14},... | collective-permute-start | bytes 2064392 | tf_op jit(solution)/shard_map/ppermute | solution.py:20
  7.2 0.5 collective-permute-start.1
  7.9 0.6 fusion.48
  8.5 13.7 %collective-permute-done.2 = f32[7,3,32,256]{3,2,1,0:T(8,128)S(1)} collective-permute-done((f32[7,3,32,256]{3,2,1,0:T(8,128)}, f32[7,3,32,256]{3,2,1,0:T(8,128)S(1)}, u32[]{:S(2)}, u32[]{:S(2)}) %collective-permute-start.2) | collective-permute-done | bytes 688160 | tf_op jit(solution)/shard_map/ppermute | solution.py:32
  22.3 13.8 %collective-permute-done.1 = f32[7,3,32,256]{3,2,1,0:T(8,128)S(1)} collective-permute-done((f32[7,3,32,256]{3,2,1,0:T(8,128)}, f32[7,3,32,256]{3,2,1,0:T(8,128)S(1)}, u32[]{:S(2)}, u32[]{:S(2)}) %collective-permute-start.1) | collective-permute-done | bytes 688160 | tf_op jit(solution)/shard_map/ppermute | solution.py:30
  36.1 1.5 %multiply_select_fusion = f32[7,3,32,256]{3,2,1,0:T(8,128)S(1)} fusion(f32[7,3,32,256]{3,2,1,0:T(8,128)S(1)} %collective-permute-done.1, f32[7,3,32,256]{3,2,1,0:T(8,128)} %collective-permute-done, f32[7]{0:T(128)S(1)} %copy-done.10, pred[]{:T(512)S(6)} %eq.25), kind=kLoop, calls=%fused_computation.37 | loop fusion | flops 344064 | bytes 2064413 | tf_op jit(solution)/shard_map/jit(_where)/select_n | solution.py:183
  37.6 1.9 %pad_maximum_fusion.2 = (f32[7,10,32,256]{3,2,1,0:T(8,128)}, f32[7,10,32,256]{3,2,1,0:T(8,128)S(1)}) fusion(f32[7,3,32,256]{3,2,1,0:T(8,128)S(1)} %broadcast_select_fusion, f32[1,4,32,256]{3,2,1,0:T(8,128)S(1)} %bitcast.49, f32[6,4,32,256]{3,2,1,0:T(8,128)S(1)} %copy-done, f32[7,3,32,256]{3,2,1,0:T(8,128)S(1)} %multiply_select_fusion, ...), kind=kLoop, calls=%fused_computation.2 | loop fusion | flops 2867200 | bytes 8257536 | tf_op jit(solution)/shard_map/concatenate | solution.py:185
  39.6 1.8 %fusion.57 = (f32[7,10,32,3]{3,2,1,0:T(8,128)}, f32[7,10,32,3]{3,2,1,0:T(8,128)}) fusion(f32[7,10,32,256]{3,2,1,0:T(8,128)S(1)} %get-tuple-element.22), kind=kLoop, calls=%fused_computation.128 | loop fusion | bytes 107520 | tf_op jit(solution)/shard_map/slice | solution.py:27
  41.3 2.6 %copy.7 = f32[7,10,32,3]{2,0,3,1:T(8,128)} copy(f32[7,10,32,3]{3,2,1,0:T(8,128)} %get-tuple-element.20) | data formatting | bytes 53760 | tf_op jit(solution)/shard_map/slice | solution.py:26
  43.9 0.3 collective-permute-start.4
  44.2 2.5 %copy.6 = f32[7,10,32,3]{2,0,3,1:T(8,128)} copy(f32[7,10,32,3]{3,2,1,0:T(8,128)} %get-tuple-element.19) | data formatting | bytes 53760 | tf_op jit(solution)/shard_map/slice | solution.py:27
  46.7 0.2 collective-permute-start.3
  47.3 0.7 add_multiply_fusion
  48.0 5.2 %add_multiply_fusion.3 = f32[6,5,32,256]{3,2,1,0:T(8,128)} fusion(f32[6,10,32,256]{3,2,1,0:T(8,128)S(1)} %get-tuple-element.16, f32[6,10,32,256]{3,2,1,0:T(8,128)S(1)} %get-tuple-element.15, f32[5]{0:T(128)S(1)} %add_convert_fusion), kind=kLoop, calls=%fused_computation.20 | loop fusion | flops 31948800 | bytes 10813460 | tf_op jit(solution)/shard_map/mul | solution.py:114
  53.2 1.4 %copy.9 = f32[7,10,32,3]{3,2,1,0:T(8,128)S(1)} copy(f32[7,10,32,3]{2,0,3,1:T(8,128)} %collective-permute-done.4) | data formatting | bytes 53760 | tf_op jit(solution)/shard_map/ppermute | solution.py:32
  54.6 1.4 %copy.8 = f32[7,10,32,3]{3,2,1,0:T(8,128)S(1)} copy(f32[7,10,32,3]{2,0,3,1:T(8,128)} %collective-permute-done.3) | data formatting | bytes 53760 | tf_op jit(solution)/shard_map/ppermute | solution.py:30
  56.0 2.6 %pad_maximum_fusion.1 = f32[7,10,32,262]{3,2,1,0:T(8,128)S(1)} fusion(f32[7,10,32,3]{3,2,1,0:T(8,128)S(1)} %copy.9, f32[7,3,32,256]{3,2,1,0:T(8,128)} %copy-done.3, f32[1,4,32,256]{3,2,1,0:T(8,128)S(1)} %bitcast.50, f32[6,4,32,256]{3,2,1,0:T(8,128)S(1)} %copy-done, f32[7,3,32,256]{3,2,1,0:T(8,128)} %copy-done.1, f32[7,10,32,3]{3,2,1,0:T(8,128)S(1)} %copy.8), kind=kLoop, calls=%fused_computation.1 | loop fusion | flops 2934400 | bytes 4695040 | tf_op jit(solution)/shard_map/concatenate | solution.py:28
  58.5 0.2 fusion.56
  58.7 0.9 copy-done.2
  59.6 0.2 copy-done.4
  59.8 0.2 multiply_dynamic-update-slice_fusion.1
  60.0 0.3 fusion.27
  60.3 0.3 fusion.26
  60.6 0.3 fusion.24
  60.9 0.3 fusion.23
  61.2 0.3 fusion.21
  61.5 0.3 add_multiply_fusion.1
  61.8 3.9 %collective-permute-start.6 = (f32[7,10,3,262]{3,2,1,0:T(4,128)S(1)}, f32[7,10,3,262]{3,2,1,0:T(4,128)S(1)}, u32[]{:S(2)}, u32[]{:S(2)}) collective-permute-start(f32[7,10,3,262]{3,2,1,0:T(4,128)S(1)} %get-tuple-element.18), channel_id=1, source_target_pairs={{1,0},{2,1},{3,2},{0,3},{5,4},{6,5},{7,6},{4,7},{9,8},{10,9},{11,1... | collective-permute-start | bytes 660248 | tf_op jit(solution)/shard_map/ppermute | solution.py:32
  65.7 5.9 %divide_add_fusion = f32[6,4,32,257]{3,2,1,0:T(8,128)S(1)} fusion(f32[6,4,32,262]{3,2,1,0:T(8,128)S(1)} %get-tuple-element.14, f32[6,4,32,262]{3,2,1,0:T(8,128)S(1)} %get-tuple-element.13), kind=kLoop, calls=%fused_computation.13 | loop fusion | flops 25461504 | bytes 8684544 | tf_op jit(solution)/shard_map/add | solution.py:103
  71.6 4.3 %collective-permute-done.6 = f32[7,10,3,262]{3,2,1,0:T(4,128)S(1)} collective-permute-done((f32[7,10,3,262]{3,2,1,0:T(4,128)S(1)}, f32[7,10,3,262]{3,2,1,0:T(4,128)S(1)}, u32[]{:S(2)}, u32[]{:S(2)}) %collective-permute-start.6) | collective-permute-done | bytes 220112 | tf_op jit(solution)/shard_map/ppermute | solution.py:32
  75.9 10.1 %collective-permute-done.5 = f32[7,10,3,262]{3,2,1,0:T(4,128)S(1)} collective-permute-done((f32[7,10,3,262]{3,2,1,0:T(4,128)S(1)}, f32[7,10,3,262]{3,2,1,0:T(4,128)S(1)}, u32[]{:S(2)}, u32[]{:S(2)}) %collective-permute-start.5) | collective-permute-done | bytes 220112 | tf_op jit(solution)/shard_map/ppermute | solution.py:30
  86.0 5.7 %pad_maximum_fusion = f32[7,10,38,262]{3,2,1,0:T(8,128)S(1)} fusion(f32[7,10,3,262]{3,2,1,0:T(4,128)S(1)} %collective-permute-done.6, f32[7,10,32,3]{3,2,1,0:T(8,128)S(1)} %copy.9, f32[7,3,32,256]{3,2,1,0:T(8,128)S(1)} %copy-done.4, f32[1,4,32,256]{3,2,1,0:T(8,128)S(1)} %bitcast.57, f32[6,4,32,256]{3,2,1,0:T(8,128)S(1)} %copy-done, ...), kind=kLoop, calls=%fused_computation | loop fusion | flops 4878440 | bytes 5575360 | tf_op jit(solution)/shard_map/concatenate | solution.py:28
  91.7 0.2 multiply_dynamic-update-slice_fusion.2
  91.9 0.1 fusion.33
  92.1 0.2 add_dynamic-update-slice_fusion.1
  92.3 0.2 fusion.31
  92.5 0.3 add_multiply_fusion.2
  92.9 5.0 %divide_add_fusion.1 = f32[6,4,33,256]{3,2,1,0:T(8,128)S(1)} fusion(f32[6,4,38,256]{3,2,1,0:T(8,128)S(1)} %get-tuple-element.12, f32[6,4,38,256]{3,2,1,0:T(8,128)S(1)} %get-tuple-element.11), kind=kLoop, calls=%fused_computation.17 | loop fusion | flops 26155008 | bytes 8921088 | tf_op jit(solution)/shard_map/add | solution.py:103
  97.9 0.7 fusion.7
  98.7 0.9 fusion.49
  99.5 0.2 collective-permute-start.7
  99.7 1.6 %collective-permute-done.7 = f32[6,4,32,128]{3,2,1,0:T(8,128)S(1)} collective-permute-done((f32[6,4,32,128]{3,2,1,0:T(8,128)S(1)}, f32[6,4,32,128]{3,2,1,0:T(8,128)S(1)}, u32[]{:S(2)}, u32[]{:S(2)}) %collective-permute-start.7) | collective-permute-done | bytes 393248 | tf_op jit(solution)/shard_map/ppermute | solution.py:160
  101.4 0.9 collective-permute-start.8
  102.5 10.1 %collective-permute-done.8 = f32[6,4,32,128]{3,2,1,0:T(8,128)S(1)} collective-permute-done((f32[6,4,32,128]{3,2,1,0:T(8,128)S(1)}, f32[6,4,32,128]{3,2,1,0:T(8,128)S(1)}, u32[]{:S(2)}, u32[]{:S(2)}) %collective-permute-start.8) | collective-permute-done | bytes 393248 | tf_op jit(solution)/shard_map/ppermute | solution.py:160
  112.6 1.7 %convolution_select_fusion = f32[6,4,32,256]{3,2,1,0:T(8,128)} fusion(f32[6,4,32,256]{3,2,1,0:T(8,128)S(1)} %fusion.7, f32[6,4,32,128]{3,2,1,0:T(8,128)S(1)} %add.582, f32[6,4,32,128]{3,2,1,0:T(8,128)S(1)} %collective-permute-done.8, pred[]{:T(512)S(6)} %eq.25, f32[4,128]{1,0:T(4,128)S(1)} %pad_maximum_fusion.8, f32[256,64]{1,0:T(8,128)S(1)} %get-tuple-element.26, ...), kind=kOutput, calls=%fused_computation.9 | convolution fusion | flops 302415872 | bytes 2492417 | tf_op jit(solution)/shard_map/vizk,tk->vizt/dot_general | solution.py:164
  (48 shorter events, 1.1 us)
Async XLA Ops:
  0.0 1.5 %copy-start = (f32[6,4,32,256]{3,2,1,0:T(8,128)S(1)}, f32[6,4,32,256]{3,2,1,0:T(8,128)}, u32[]{:S(2)}) copy-start(f32[6,4,32,256]{3,2,1,0:T(8,128)} %param.6) | copy-start | bytes 2359300
  2.7 19.5 %collective-permute-start.2 = (f32[7,3,32,256]{3,2,1,0:T(8,128)}, f32[7,3,32,256]{3,2,1,0:T(8,128)S(1)}, u32[]{:S(2)}, u32[]{:S(2)}) collective-permute-start(f32[7,3,32,256]{3,2,1,0:T(8,128)} %get-tuple-element.24), channel_id=1, source_target_pairs={{16,0},{0,16},{17,1},{1,17},{18,2},{2,18},{19,3},{3,19},{20,4},{4,... | collective-permute-start | bytes 2064392 | tf_op jit(solution)/shard_map/ppermute | solution.py:32
  5.7 30.4 %collective-permute-start = (f32[7,3,32,256]{3,2,1,0:T(8,128)}, f32[7,3,32,256]{3,2,1,0:T(8,128)}, u32[]{:S(2)}, u32[]{:S(2)}) collective-permute-start(f32[7,3,32,256]{3,2,1,0:T(8,128)} %get-tuple-element.24), channel_id=1, source_target_pairs={{0,8},{4,12},{8,0},{12,4},{1,9},{5,13},{9,1},{13,5},{2,10},{6,14},... | collective-permute-start | bytes 2064392 | tf_op jit(solution)/shard_map/ppermute | solution.py:20
  7.2 28.9 %collective-permute-start.1 = (f32[7,3,32,256]{3,2,1,0:T(8,128)}, f32[7,3,32,256]{3,2,1,0:T(8,128)S(1)}, u32[]{:S(2)}, u32[]{:S(2)}) collective-permute-start(f32[7,3,32,256]{3,2,1,0:T(8,128)} %get-tuple-element.23), channel_id=1, source_target_pairs={{0,16},{16,0},{1,17},{17,1},{2,18},{18,2},{3,19},{19,3},{4,20},{20... | collective-permute-start | bytes 2064392 | tf_op jit(solution)/shard_map/ppermute | solution.py:30
  7.8 28.3 %copy-start.10 = (f32[7]{0:T(128)S(1)}, f32[7]{0:T(128)}, u32[]{:S(2)}) copy-start(f32[7]{0:T(128)} %constant.69.clone) | copy-start | bytes 88
  7.9 29.7 %copy-start.7 = (f32[6,4,32,256]{3,2,1,0:T(8,128)}, f32[6,4,32,256]{3,2,1,0:T(8,128)S(1)}, u32[]{:S(2)}) copy-start(f32[6,4,32,256]{3,2,1,0:T(8,128)S(1)} %broadcast_dynamic-update-slice_fusion) | copy-start | bytes 2359300
  22.2 15.4 %copy-start.3 = (f32[7,3,32,256]{3,2,1,0:T(8,128)}, f32[7,3,32,256]{3,2,1,0:T(8,128)S(1)}, u32[]{:S(2)}) copy-start(f32[7,3,32,256]{3,2,1,0:T(8,128)S(1)} %collective-permute-done.2) | copy-start | bytes 2064388
  36.1 3.5 %copy-start.1 = (f32[7,3,32,256]{3,2,1,0:T(8,128)}, f32[7,3,32,256]{3,2,1,0:T(8,128)S(1)}, u32[]{:S(2)}) copy-start(f32[7,3,32,256]{3,2,1,0:T(8,128)S(1)} %collective-permute-done.1) | copy-start | bytes 2064388
  41.3 5.6 %copy-start.5 = (f32[7,10,32,256]{3,2,1,0:T(8,128)S(1)}, f32[7,10,32,256]{3,2,1,0:T(8,128)}, u32[]{:S(2)}) copy-start(f32[7,10,32,256]{3,2,1,0:T(8,128)} %get-tuple-element.21) | copy-start | bytes 6881284
  43.9 9.3 %collective-permute-start.4 = (f32[7,10,32,3]{2,0,3,1:T(8,128)}, f32[7,10,32,3]{2,0,3,1:T(8,128)}, u32[]{:S(2)}, u32[]{:S(2)}) collective-permute-start(f32[7,10,32,3]{2,0,3,1:T(8,128)} %copy.7), channel_id=1, source_target_pairs={{4,0},{8,4},{12,8},{0,12},{5,1},{9,5},{13,9},{1,13},{6,2},{10,6},{... | collective-permute-start | bytes 80648 | tf_op jit(solution)/shard_map/ppermute | solution.py:32
  46.7 7.9 %collective-permute-start.3 = (f32[7,10,32,3]{2,0,3,1:T(8,128)}, f32[7,10,32,3]{2,0,3,1:T(8,128)}, u32[]{:S(2)}, u32[]{:S(2)}) collective-permute-start(f32[7,10,32,3]{2,0,3,1:T(8,128)} %copy.6), channel_id=1, source_target_pairs={{0,4},{4,8},{8,12},{12,0},{1,5},{5,9},{9,13},{13,1},{2,6},{6,10},{... | collective-permute-start | bytes 80648 | tf_op jit(solution)/shard_map/ppermute | solution.py:30
  58.5 1.1 copy-start.2
  58.5 1.3 %copy-start.4 = (f32[7,3,32,256]{3,2,1,0:T(8,128)S(1)}, f32[7,3,32,256]{3,2,1,0:T(8,128)}, u32[]{:S(2)}) copy-start(f32[7,3,32,256]{3,2,1,0:T(8,128)} %copy-done.3) | copy-start | bytes 2064388
  61.8 14.1 %collective-permute-start.6 = (f32[7,10,3,262]{3,2,1,0:T(4,128)S(1)}, f32[7,10,3,262]{3,2,1,0:T(4,128)S(1)}, u32[]{:S(2)}, u32[]{:S(2)}) collective-permute-start(f32[7,10,3,262]{3,2,1,0:T(4,128)S(1)} %get-tuple-element.18), channel_id=1, source_target_pairs={{1,0},{2,1},{3,2},{0,3},{5,4},{6,5},{7,6},{4,7},{9,8},{10,9},{11,1... | collective-permute-start | bytes 660248 | tf_op jit(solution)/shard_map/ppermute | solution.py:32
  65.7 20.3 %collective-permute-start.5 = (f32[7,10,3,262]{3,2,1,0:T(4,128)S(1)}, f32[7,10,3,262]{3,2,1,0:T(4,128)S(1)}, u32[]{:S(2)}, u32[]{:S(2)}) collective-permute-start(f32[7,10,3,262]{3,2,1,0:T(4,128)S(1)} %get-tuple-element.17), channel_id=1, source_target_pairs={{0,1},{1,2},{2,3},{3,0},{4,5},{5,6},{6,7},{7,4},{8,9},{9,10},{10,1... | collective-permute-start | bytes 660248 | tf_op jit(solution)/shard_map/ppermute | solution.py:30
  92.9 5.0 %copy-start.6 = (f32[6,5,32,256]{3,2,1,0:T(8,128)S(1)}, f32[6,5,32,256]{3,2,1,0:T(8,128)}, u32[]{:S(2)}) copy-start(f32[6,5,32,256]{3,2,1,0:T(8,128)} %add_multiply_fusion.3) | copy-start | bytes 2949124
  92.9 5.0 %copy-start.8 = (f32[6,4,32,256]{3,2,1,0:T(8,128)S(1)}, f32[6,4,32,256]{3,2,1,0:T(8,128)}, u32[]{:S(2)}) copy-start(f32[6,4,32,256]{3,2,1,0:T(8,128)} %copy-done.7) | copy-start | bytes 2359300
  92.9 5.0 %copy-start.9 = (f32[6,4,32,256]{3,2,1,0:T(8,128)S(1)}, f32[6,4,32,256]{3,2,1,0:T(8,128)}, u32[]{:S(2)}) copy-start(f32[6,4,32,256]{3,2,1,0:T(8,128)} %param.5) | copy-start | bytes 2359300
  98.7 3.7 %copy-start.11 = (s32[4]{0:T(128)S(1)}, s32[4]{0:T(128)}, u32[]{:S(2)}) copy-start(s32[4]{0:T(128)} %param.8) | copy-start | bytes 52
  99.5 1.8 %collective-permute-start.7 = (f32[6,4,32,128]{3,2,1,0:T(8,128)S(1)}, f32[6,4,32,128]{3,2,1,0:T(8,128)S(1)}, u32[]{:S(2)}, u32[]{:S(2)}) collective-permute-start(f32[6,4,32,128]{3,2,1,0:T(8,128)S(1)} %fusion.49), channel_id=1, source_target_pairs={{0,4},{4,0},{8,12},{12,8},{1,5},{5,1},{9,13},{13,9},{2,6},{6,2},{1... | collective-permute-start | bytes 1179656 | tf_op jit(solution)/shard_map/ppermute | solution.py:160
  101.4 11.2 %collective-permute-start.8 = (f32[6,4,32,128]{3,2,1,0:T(8,128)S(1)}, f32[6,4,32,128]{3,2,1,0:T(8,128)S(1)}, u32[]{:S(2)}, u32[]{:S(2)}) collective-permute-start(f32[6,4,32,128]{3,2,1,0:T(8,128)S(1)} %add.582), channel_id=1, source_target_pairs={{0,8},{4,12},{8,0},{12,4},{1,9},{5,13},{9,1},{13,5},{2,10},{6,14},... | collective-permute-start | bytes 1179656 | tf_op jit(solution)/shard_map/ppermute | solution.py:160
